TPU v7x, 32 devices: a whole 2x2x4 slice. The times are simulated.
32 devices in a mesh: tile: 8 (over z, x), dir: 4 (over y, core).
Axes of the slice: x: 2, y: 2, z: 4, core: 2. Of those that a mesh axis runs over, the one named last changes fastest.
Arguments:
- probes: float32 [32, 64, 32, 128], P('dir', 'tile'), may hold values from -6 to 6
- base_sens: float32 [64, 32, 128], P('tile'), may hold values from -12 to 12
- obs_weight: float32 [64, 32, 128], P('tile'), may hold values from 1 to 10
- perm: float32 [64, 32, 128], P('tile'), may hold values from 0.25 to 4
- material: int32 [64, 32, 128], P('tile'), may hold values from 0 to 7
- class_storage: float32 [8], replicated, may hold values from 0.2 to 2
- class_alpha: float32 [8], replicated, may hold values from 0.5 to 1
- class_bulk: float32 [8], replicated, may hold values from 0.25 to 2
- class_shear: float32 [8], replicated, may hold values from 0.5 to 4
Outputs:
- hess_block: float32 [32, 64, 32, 128], P('dir', 'tile')
- r_factor: float32 [32, 32], replicated
All inputs are finite; a program needn't handle non-finite values.
Results may differ from a plain program's by a relative error of at most 0.00016.
Values sent between devices are 32-bit elements; how exact they have to be, the bound alone decides.
A program may use at most 64 MiB of HBM per device.

v0:
```python
import jax
import jax.numpy as jnp
from jax import lax
from jax.sharding import PartitionSpec as P

NCLASS = 8
SWEEPS = 2
STEPS = 2


def extended(cells, sides, width):
    for axis, dim in sides:
        count = lax.axis_size(axis)
        ends = count - 1
        head = lax.slice_in_dim(cells, 0, width, axis=dim)
        tail = lax.slice_in_dim(cells, cells.shape[dim] - width, cells.shape[dim], axis=dim)
        cells = jnp.concatenate(
            [
                lax.ppermute(tail, axis, [(i, (i + 1) % count) for i in range(ends)]),
                cells,
                lax.ppermute(head, axis, [((i + 1) % count, i) for i in range(ends)]),
            ],
            axis=dim,
        )
    return cells


def pad_second(field):
    return jnp.pad(field, [(0, 0)] * (field.ndim - 2) + [(1, 1), (0, 0)])


def pad_third(field):
    return jnp.pad(field, [(0, 0)] * (field.ndim - 1) + [(1, 1)])


def face_flux(padded, coef_pad):
    center = padded[..., 1:-1, :, :]
    coef_mid = coef_pad[1:-1]
    result = 0.5 * (coef_mid + coef_pad[2:]) * (center - padded[..., 2:, :, :])
    result = result + 0.5 * (coef_mid + coef_pad[:-2]) * (center - padded[..., :-2, :, :])
    field_y = pad_second(center)
    coef_y = pad_second(coef_mid)
    result = result + 0.5 * (coef_mid + coef_y[:, 2:]) * (center - field_y[..., 2:, :])
    result = result + 0.5 * (coef_mid + coef_y[:, :-2]) * (center - field_y[..., :-2, :])
    field_z = pad_third(center)
    coef_z = pad_third(coef_mid)
    result = result + 0.5 * (coef_mid + coef_z[:, :, 2:]) * (center - field_z[..., 2:])
    result = result + 0.5 * (coef_mid + coef_z[:, :, :-2]) * (center - field_z[..., :-2])
    return result


def gradient(press_pad, biot):
    first = 0.5 * biot * (press_pad[..., 2:, :, :] - press_pad[..., :-2, :, :])
    center = press_pad[..., 1:-1, :, :]
    field_y = pad_second(center)
    second = 0.5 * biot * (field_y[..., 2:, :] - field_y[..., :-2, :])
    field_z = pad_third(center)
    third = 0.5 * biot * (field_z[..., 2:] - field_z[..., :-2])
    return jnp.stack([first, second, third])


def divergence(first_pad, others, biot_pad):
    weighted = biot_pad * first_pad
    result = 0.5 * (weighted[..., :-2, :, :] - weighted[..., 2:, :, :])
    biot = biot_pad[1:-1]
    second = pad_second(biot * others[0])
    result = result + 0.5 * (second[..., :-2, :] - second[..., 2:, :])
    third = pad_third(biot * others[1])
    result = result + 0.5 * (third[..., :-2] - third[..., 2:])
    return result


def inner(left, right):
    summed = jnp.sum(left * right, axis=(-3, -2, -1))
    if summed.ndim == 2:
        summed = jnp.sum(summed, axis=0)
    return lax.psum(summed, "tile")


def spread(values):
    return values[:, None, None, None]


def pad_scalar(field):
    return extended(field, (("tile", 1),), 1)


def pad_vector(field):
    return extended(field, (("tile", 2),), 1)


def conj_grad(operate, extend, target, iterate, iter_pad):
    if iterate is None:
        residual = target
        iterate = jnp.zeros_like(target)
    else:
        residual = target - operate(iter_pad)
    direction = residual
    norm_now = inner(residual, residual)
    for step in range(STEPS):
        image = operate(extend(direction))
        step_len = norm_now / inner(direction, image)
        iterate = iterate + spread(step_len) * direction
        if step + 1 < STEPS:
            residual = residual - spread(step_len) * image
            norm_next = inner(residual, residual)
            direction = residual + spread(norm_next / norm_now) * direction
            norm_now = norm_next
    return iterate


def body(
    probes,
    base_sens,
    obs_weight,
    perm,
    material,
    class_storage,
    class_alpha,
    class_bulk,
    class_shear,
):
    class_mask = (
        material[None] == jnp.arange(NCLASS, dtype=jnp.int32)[:, None, None, None]
    ).astype(jnp.float32)
    storage = jnp.sum(class_storage[:, None, None, None] * class_mask, axis=0)
    biot = jnp.sum(class_alpha[:, None, None, None] * class_mask, axis=0)
    bulk = jnp.sum(class_bulk[:, None, None, None] * class_mask, axis=0)
    shear = jnp.sum(class_shear[:, None, None, None] * class_mask, axis=0)
    stab_term = biot * biot / bulk
    diagonal = storage + stab_term
    coef_all = extended(jnp.stack([perm, biot, shear]), (("tile", 1),), 1)
    perm_pad = coef_all[0]
    biot_pad = coef_all[1]
    shear_pad = coef_all[2]

    def press_apply(padded):
        return diagonal * padded[..., 1:-1, :, :] + face_flux(padded, perm_pad)

    def elast_apply(padded):
        return face_flux(padded, shear_pad)

    def solve(source, orient):
        pressure = None
        displace = None
        press_pad = None
        for sweep in range(SWEEPS):
            source_term = source
            press_init = None
            disp_pad = None
            if displace is not None:
                first_pad = pad_scalar(displace[0])
                press_init = pad_scalar(pressure)
                source_term = (
                    source
                    - orient * divergence(first_pad, (displace[1], displace[2]), biot_pad)
                    + stab_term * pressure
                )
            pressure = conj_grad(press_apply, pad_scalar, source_term, pressure, press_init)
            press_pad = pad_scalar(pressure)
            elastic_term = orient * gradient(press_pad, biot)
            if displace is not None and disp_pad is None:
                disp_pad = pad_vector(displace)
            displace = conj_grad(elast_apply, pad_vector, elastic_term, displace, disp_pad)
        return pressure

    tangent = solve(base_sens * probes, 1.0)
    adjoint = solve(obs_weight * tangent, -1.0)
    hess_block = base_sens * adjoint
    cell_count = (
        hess_block.shape[1] * lax.axis_size("tile") * hess_block.shape[2] * hess_block.shape[3]
    )
    regrouped = lax.all_to_all(hess_block, "dir", split_axis=2, concat_axis=0, tiled=True)
    columns = regrouped.reshape(regrouped.shape[0], -1)
    gram_local = (
        jnp.dot(
            columns, columns.T, precision=lax.Precision.HIGHEST, preferred_element_type=jnp.float32
        )
        / cell_count
    )
    gram_whole = lax.psum(gram_local, ("tile", "dir"))
    r_factor = jnp.linalg.cholesky(gram_whole).T
    return (hess_block, r_factor)


def solution(mesh):
    placed = (
        P("dir", "tile", None, None),
        P("tile", None, None),
        P("tile", None, None),
        P("tile", None, None),
        P("tile", None, None),
        P(),
        P(),
        P(),
        P(),
    )
    return jax.shard_map(
        body,
        mesh=mesh,
        in_specs=placed,
        out_specs=(P("dir", "tile", None, None), P()),
        check_vma=False,
    )
```

profile of v0, /device:TPU:0, one launch (start us, length us, event | category | flops | bytes accessed | tf_op | source)
XLA Modules:
  0.0 663.4 jit_solution(10899361702764466490)
XLA Ops:
  4.2 5.5 collective-permute-start.2
  12.5 5.5 collective-permute-start.3
  23.1 21.0 %all-reduce.41 = (f32[8]{0:T(128)S(1)}, f32[8]{0:T(128)S(1)}) all-reduce(f32[8]{0:T(128)S(1)} %get-tuple-element.23, f32[8]{0:T(128)S(1)} %get-tuple-element.22), channel_id=1, replica_groups=mesh['tile'=8,'dir'=4] {'tile'}, use_global_device_ids=true, to_apply=%region_1.0 | all-reduce | flops 16 | bytes 128 | tf_op jit(solution)/shard_map/psum | solution.py:77
  44.5 17.3 %psum.177 = f32[8]{0:T(128)S(1)} all-reduce(f32[8]{0:T(128)S(1)} %multiply_reduce_fusion.15), channel_id=1, replica_groups=mesh['tile'=8,'dir'=4] {'tile'}, use_global_device_ids=true, to_apply=%region_9.10 | all-reduce | flops 8 | bytes 64 | tf_op jit(solution)/shard_map/psum | solution.py:77
  64.7 4.6 collective-permute-start.5
  73.2 19.7 %psum.178 = f32[8]{0:T(128)S(1)} all-reduce(f32[8]{0:T(128)S(1)} %fusion.269), channel_id=1, replica_groups=mesh['tile'=8,'dir'=4] {'tile'}, use_global_device_ids=true, to_apply=%region_11.12 | all-reduce | flops 8 | bytes 64 | tf_op jit(solution)/shard_map/psum | solution.py:77
  94.6 4.6 collective-permute-start.7
  106.8 5.0 collective-permute-start.9
  112.1 3.5 collective-permute-done.8
  115.7 4.9 collective-permute-done.9
  120.5 4.5 multiply_reduce_fusion.4
  125.1 19.6 %all-reduce.40 = (f32[8]{0:T(128)S(1)}, f32[8]{0:T(128)S(1)}) all-reduce(f32[8]{0:T(128)S(1)} %get-tuple-element.15, f32[8]{0:T(128)S(1)} %get-tuple-element.14), channel_id=1, replica_groups=mesh['tile'=8,'dir'=4] {'tile'}, use_global_device_ids=true, to_apply=%region_13.14 | all-reduce | flops 16 | bytes 128 | tf_op jit(solution)/shard_map/psum | solution.py:77
  147.2 17.2 %psum.181 = f32[8]{0:T(128)S(1)} all-reduce(f32[8]{0:T(128)S(1)} %multiply_reduce_fusion.3), channel_id=1, replica_groups=mesh['tile'=8,'dir'=4] {'tile'}, use_global_device_ids=true, to_apply=%region_17.18 | all-reduce | flops 8 | bytes 64 | tf_op jit(solution)/shard_map/psum | solution.py:77
  168.8 4.6 collective-permute-start.11
  173.4 3.9 collective-permute-done.10
  177.3 4.6 collective-permute-done.11
  181.9 3.5 fusion.71
  186.1 20.3 %psum.182 = f32[8]{0:T(128)} all-reduce(f32[8]{0:T(128)S(1)} %fusion.71), channel_id=1, replica_groups=mesh['tile'=8,'dir'=4] {'tile'}, use_global_device_ids=true, to_apply=%region_19.20 | all-reduce | flops 8 | bytes 64 | tf_op jit(solution)/shard_map/psum | solution.py:77
  214.0 4.7 collective-permute-done.13
  222.5 4.6 collective-permute-start.15
  232.1 19.7 %all-reduce.39 = (f32[8]{0:T(128)S(1)}, f32[8]{0:T(128)S(1)}) all-reduce(f32[8]{0:T(128)S(1)} %get-tuple-element.21, f32[8]{0:T(128)S(1)} %get-tuple-element.20), channel_id=1, replica_groups=mesh['tile'=8,'dir'=4] {'tile'}, use_global_device_ids=true, to_apply=%region_21.22 | all-reduce | flops 16 | bytes 128 | tf_op jit(solution)/shard_map/psum | solution.py:77
  253.3 17.6 %psum.185 = f32[8]{0:T(128)S(1)} all-reduce(f32[8]{0:T(128)S(1)} %multiply_reduce_fusion.12), channel_id=1, replica_groups=mesh['tile'=8,'dir'=4] {'tile'}, use_global_device_ids=true, to_apply=%region_25.26 | all-reduce | flops 8 | bytes 64 | tf_op jit(solution)/shard_map/psum | solution.py:77
  273.8 4.6 collective-permute-start.17
  282.1 19.6 %psum.186 = f32[8]{0:T(128)S(1)} all-reduce(f32[8]{0:T(128)S(1)} %fusion.268), channel_id=1, replica_groups=mesh['tile'=8,'dir'=4] {'tile'}, use_global_device_ids=true, to_apply=%region_27.28 | all-reduce | flops 8 | bytes 64 | tf_op jit(solution)/shard_map/psum | solution.py:77
  304.8 4.6 collective-permute-start.19
  315.9 19.7 %all-reduce.38 = (f32[8]{0:T(128)S(1)}, f32[8]{0:T(128)S(1)}) all-reduce(f32[8]{0:T(128)S(1)} %get-tuple-element.19, f32[8]{0:T(128)S(1)} %get-tuple-element.18), channel_id=1, replica_groups=mesh['tile'=8,'dir'=4] {'tile'}, use_global_device_ids=true, to_apply=%region_29.30 | all-reduce | flops 16 | bytes 128 | tf_op jit(solution)/shard_map/psum | solution.py:77
  336.0 17.2 %psum.189 = f32[8]{0:T(128)S(1)} all-reduce(f32[8]{0:T(128)S(1)} %multiply_reduce_fusion.9), channel_id=1, replica_groups=mesh['tile'=8,'dir'=4] {'tile'}, use_global_device_ids=true, to_apply=%region_33.34 | all-reduce | flops 8 | bytes 64 | tf_op jit(solution)/shard_map/psum | solution.py:77
  356.2 4.6 collective-permute-start.21
  364.9 19.7 %psum.190 = f32[8]{0:T(128)S(1)} all-reduce(f32[8]{0:T(128)S(1)} %fusion.267), channel_id=1, replica_groups=mesh['tile'=8,'dir'=4] {'tile'}, use_global_device_ids=true, to_apply=%region_35.36 | all-reduce | flops 8 | bytes 64 | tf_op jit(solution)/shard_map/psum | solution.py:77
  386.2 4.6 collective-permute-start.23
  396.4 5.2 collective-permute-start.25
  401.6 7.0 %collective-permute-done.24 = f32[3,8,1,32,128]{4,3,2,1,0:T(8,128)S(1)} collective-permute-done((f32[3,8,1,32,128]{4,3,2,1,0:T(8,128)S(1)}, f32[3,8,1,32,128]{4,3,2,1,0:T(8,128)S(1)}, u32[]{:S(2)}, u32[]{:S(2)}) %collective-permute-start.24) | collective-permute-done | bytes 393248 | tf_op jit(solution)/shard_map/ppermute | solution.py:21
  408.7 8.6 %collective-permute-done.25 = f32[3,8,1,32,128]{4,3,2,1,0:T(8,128)S(1)} collective-permute-done((f32[3,8,1,32,128]{4,3,2,1,0:T(8,128)S(1)}, f32[3,8,1,32,128]{4,3,2,1,0:T(8,128)S(1)}, u32[]{:S(2)}, u32[]{:S(2)}) %collective-permute-start.25) | collective-permute-done | bytes 393248 | tf_op jit(solution)/shard_map/ppermute | solution.py:19
  417.3 4.6 multiply_reduce_fusion.1
  421.9 20.1 %all-reduce.37 = (f32[8]{0:T(128)S(1)}, f32[8]{0:T(128)}) all-reduce(f32[8]{0:T(128)S(1)} %get-tuple-element.13, f32[8]{0:T(128)S(1)} %get-tuple-element.12), channel_id=1, replica_groups=mesh['tile'=8,'dir'=4] {'tile'}, use_global_device_ids=true, to_apply=%region_37.38 | all-reduce | flops 16 | bytes 128 | tf_op jit(solution)/shard_map/psum | solution.py:77
  445.2 17.7 %psum.193 = f32[8]{0:T(128)} all-reduce(f32[8]{0:T(128)S(1)} %multiply_reduce_fusion), channel_id=1, replica_groups=mesh['tile'=8,'dir'=4] {'tile'}, use_global_device_ids=true, to_apply=%region_41.42 | all-reduce | flops 8 | bytes 64 | tf_op jit(solution)/shard_map/psum | solution.py:77
  467.8 4.6 collective-permute-start.27
  472.4 3.8 collective-permute-done.26
  476.2 4.5 collective-permute-done.27
  484.3 20.2 %psum.194 = f32[8]{0:T(128)} all-reduce(f32[8]{0:T(128)S(1)} %fusion.70), channel_id=1, replica_groups=mesh['tile'=8,'dir'=4] {'tile'}, use_global_device_ids=true, to_apply=%region_43.44 | all-reduce | flops 8 | bytes 64 | tf_op jit(solution)/shard_map/psum | solution.py:77
  512.1 4.7 collective-permute-done.29
  520.4 4.6 collective-permute-start.31
  529.5 20.2 %all-reduce.36 = (f32[8]{0:T(128)S(1)}, f32[8]{0:T(128)S(1)}) all-reduce(f32[8]{0:T(128)S(1)} %get-tuple-element.17, f32[8]{0:T(128)S(1)} %get-tuple-element.16), channel_id=1, replica_groups=mesh['tile'=8,'dir'=4] {'tile'}, use_global_device_ids=true, to_apply=%region_45.46 | all-reduce | flops 16 | bytes 128 | tf_op jit(solution)/shard_map/psum | solution.py:77
  551.3 17.4 %psum.197 = f32[8]{0:T(128)S(1)} all-reduce(f32[8]{0:T(128)S(1)} %multiply_reduce_fusion.6), channel_id=1, replica_groups=mesh['tile'=8,'dir'=4] {'tile'}, use_global_device_ids=true, to_apply=%region_49.50 | all-reduce | flops 8 | bytes 64 | tf_op jit(solution)/shard_map/psum | solution.py:77
  571.6 4.6 collective-permute-start.33
  579.9 19.7 %psum.198 = f32[8]{0:T(128)S(1)} all-reduce(f32[8]{0:T(128)S(1)} %fusion.266), channel_id=1, replica_groups=mesh['tile'=8,'dir'=4] {'tile'}, use_global_device_ids=true, to_apply=%region_51.52 | all-reduce | flops 8 | bytes 64 | tf_op jit(solution)/shard_map/psum | solution.py:77
  601.9 17.3 %all_to_all.15 = f32[8,8,32,128]{3,1,0,2:T(8,128)S(1)} all-to-all(f32[8,8,32,128]{3,1,0,2:T(8,128)S(1)} %copy.48), channel_id=1, replica_groups=mesh['tile'=8,'dir'=4] {'dir'}, dimensions={2} | all-to-all | bytes 2097152 | tf_op jit(solution)/shard_map/all_to_all | solution.py:173
  621.0 36.9 %psum.199 = f32[32,32]{0,1:T(8,128)S(1)} all-reduce(f32[32,32]{0,1:T(8,128)S(1)} %convolution_multiply_fusion), channel_id=1, replica_groups=mesh['tile'=8,'dir'=4] {'tile','dir'}, use_global_device_ids=true, to_apply=%region_52.53 | all-reduce | flops 1024 | bytes 8192 | tf_op jit(solution)/shard_map/psum | solution.py:181
  (312 shorter events, 128.1 us)
Async XLA Ops:
  2.0 109.9 %copy-start.34 = (f32[8,32,128]{2,1,0:T(8,128)}, f32[8,32,128]{2,1,0:T(8,128)S(1)}, u32[]{:S(2)}) copy-start(f32[8,32,128]{2,1,0:T(8,128)S(1)} %get-tuple-element.26) | copy-start | bytes 393220
  2.0 109.9 %copy-start.41 = (f32[8,32,128]{2,1,0:T(8,128)}, f32[8,32,128]{2,1,0:T(8,128)S(1)}, u32[]{:S(2)}) copy-start(f32[8,32,128]{2,1,0:T(8,128)S(1)} %get-tuple-element.25) | copy-start | bytes 393220
  2.9 15.9 %collective-permute-start = (f32[3,1,32,128]{3,2,1,0:T(8,128)S(1)}, f32[3,1,32,128]{3,2,1,0:T(8,128)S(1)}, u32[]{:S(2)}, u32[]{:S(2)}) collective-permute-start(f32[3,1,32,128]{3,2,1,0:T(8,128)S(1)} %get-tuple-element.96), channel_id=1, source_target_pairs={{4,0},{8,4},{12,8},{16,12},{20,16},{24,20},{28,24},{5,1},{9,5},{13... | collective-permute-start | bytes 147464 | tf_op jit(solution)/shard_map/ppermute | solution.py:21
  4.2 14.7 %collective-permute-start.2 = (f32[3,1,32,128]{3,2,1,0:T(8,128)S(1)}, f32[3,1,32,128]{3,2,1,0:T(8,128)S(1)}, u32[]{:S(2)}, u32[]{:S(2)}) collective-permute-start(f32[3,1,32,128]{3,2,1,0:T(8,128)S(1)} %get-tuple-element.97), channel_id=1, source_target_pairs={{0,4},{4,8},{8,12},{12,16},{16,20},{20,24},{24,28},{1,5},{5,9},{9,... | collective-permute-start | bytes 147464 | tf_op jit(solution)/shard_map/ppermute | solution.py:19
  11.1 7.9 %collective-permute-start.1 = (f32[8,1,32,128]{3,2,1,0:T(8,128)S(1)}, f32[8,1,32,128]{3,2,1,0:T(8,128)S(1)}, u32[]{:S(2)}, u32[]{:S(2)}) collective-permute-start(f32[8,1,32,128]{3,2,1,0:T(8,128)S(1)} %get-tuple-element.90), channel_id=1, source_target_pairs={{4,0},{8,4},{12,8},{16,12},{20,16},{24,20},{28,24},{5,1},{9,5},{13... | collective-permute-start | bytes 393224 | tf_op jit(solution)/shard_map/ppermute | solution.py:21
  12.5 9.4 %collective-permute-start.3 = (f32[8,1,32,128]{3,2,1,0:T(8,128)S(1)}, f32[8,1,32,128]{3,2,1,0:T(8,128)S(1)}, u32[]{:S(2)}, u32[]{:S(2)}) collective-permute-start(f32[8,1,32,128]{3,2,1,0:T(8,128)S(1)} %get-tuple-element.91), channel_id=1, source_target_pairs={{0,4},{4,8},{8,12},{12,16},{16,20},{20,24},{24,28},{1,5},{5,9},{9,... | collective-permute-start | bytes 393224 | tf_op jit(solution)/shard_map/ppermute | solution.py:19
  18.8 53.3 %copy-start.14 = (f32[8,32,128]{2,1,0:T(8,128)}, f32[8,32,128]{2,1,0:T(8,128)S(1)}, u32[]{:S(2)}) copy-start(f32[8,32,128]{2,1,0:T(8,128)S(1)} %get-tuple-element.104) | copy-start | bytes 393220
  18.8 53.3 %copy-start.18 = (f32[8,32,128]{2,1,0:T(8,128)}, f32[8,32,128]{2,1,0:T(8,128)S(1)}, u32[]{:S(2)}) copy-start(f32[8,32,128]{2,1,0:T(8,128)S(1)} %get-tuple-element.105) | copy-start | bytes 393220
  18.8 53.3 %copy-start.22 = (f32[8,32,128]{2,1,0:T(8,128)}, f32[8,32,128]{2,1,0:T(8,128)S(1)}, u32[]{:S(2)}) copy-start(f32[8,32,128]{2,1,0:T(8,128)S(1)} %get-tuple-element.106) | copy-start | bytes 393220
  18.8 53.3 %copy-start.26 = (f32[8,32,128]{2,1,0:T(8,128)}, f32[8,32,128]{2,1,0:T(8,128)S(1)}, u32[]{:S(2)}) copy-start(f32[8,32,128]{2,1,0:T(8,128)S(1)} %get-tuple-element.108) | copy-start | bytes 393220
  23.1 38.7 %copy-start.32 = (f32[8,8,32,128]{3,2,1,0:T(8,128)}, f32[8,8,32,128]{3,2,1,0:T(8,128)S(1)}, u32[]{:S(2)}) copy-start(f32[8,8,32,128]{3,2,1,0:T(8,128)S(1)} %get-tuple-element.47) | copy-start | bytes 3145732
  63.4 6.9 %collective-permute-start.4 = (f32[8,1,32,128]{3,2,1,0:T(8,128)S(1)}, f32[8,1,32,128]{3,2,1,0:T(8,128)S(1)}, u32[]{:S(2)}, u32[]{:S(2)}) collective-permute-start(f32[8,1,32,128]{3,2,1,0:T(8,128)S(1)} %get-tuple-element.88), channel_id=1, source_target_pairs={{4,0},{8,4},{12,8},{16,12},{20,16},{24,20},{28,24},{5,1},{9,5},{13... | collective-permute-start | bytes 393224 | tf_op jit(solution)/shard_map/ppermute | solution.py:21
  64.7 7.4 %collective-permute-start.5 = (f32[8,1,32,128]{3,2,1,0:T(8,128)S(1)}, f32[8,1,32,128]{3,2,1,0:T(8,128)S(1)}, u32[]{:S(2)}, u32[]{:S(2)}) collective-permute-start(f32[8,1,32,128]{3,2,1,0:T(8,128)S(1)} %get-tuple-element.89), channel_id=1, source_target_pairs={{0,4},{4,8},{8,12},{12,16},{16,20},{20,24},{24,28},{1,5},{5,9},{9,... | collective-permute-start | bytes 393224 | tf_op jit(solution)/shard_map/ppermute | solution.py:19
  93.3 6.9 %collective-permute-start.6 = (f32[8,1,32,128]{3,2,1,0:T(8,128)S(1)}, f32[8,1,32,128]{3,2,1,0:T(8,128)S(1)}, u32[]{:S(2)}, u32[]{:S(2)}) collective-permute-start(f32[8,1,32,128]{3,2,1,0:T(8,128)S(1)} %get-tuple-element.86), channel_id=1, source_target_pairs={{4,0},{8,4},{12,8},{16,12},{20,16},{24,20},{28,24},{5,1},{9,5},{13... | collective-permute-start | bytes 393224 | tf_op jit(solution)/shard_map/ppermute | solution.py:21
  94.6 8.4 %collective-permute-start.7 = (f32[8,1,32,128]{3,2,1,0:T(8,128)S(1)}, f32[8,1,32,128]{3,2,1,0:T(8,128)S(1)}, u32[]{:S(2)}, u32[]{:S(2)}) collective-permute-start(f32[8,1,32,128]{3,2,1,0:T(8,128)S(1)} %get-tuple-element.87), channel_id=1, source_target_pairs={{0,4},{4,8},{8,12},{12,16},{16,20},{20,24},{24,28},{1,5},{5,9},{9,... | collective-permute-start | bytes 393224 | tf_op jit(solution)/shard_map/ppermute | solution.py:19
  105.5 10.1 %collective-permute-start.8 = (f32[3,8,1,32,128]{4,3,2,1,0:T(8,128)S(1)}, f32[3,8,1,32,128]{4,3,2,1,0:T(8,128)S(1)}, u32[]{:S(2)}, u32[]{:S(2)}) collective-permute-start(f32[3,8,1,32,128]{4,3,2,1,0:T(8,128)S(1)} %get-tuple-element.60), channel_id=1, source_target_pairs={{4,0},{8,4},{12,8},{16,12},{20,16},{24,20},{28,24},{5,1},{9,5},{13... | collective-permute-start | bytes 1179656 | tf_op jit(solution)/shard_map/ppermute | solution.py:21
  106.8 13.7 %collective-permute-start.9 = (f32[3,8,1,32,128]{4,3,2,1,0:T(8,128)S(1)}, f32[3,8,1,32,128]{4,3,2,1,0:T(8,128)S(1)}, u32[]{:S(2)}, u32[]{:S(2)}) collective-permute-start(f32[3,8,1,32,128]{4,3,2,1,0:T(8,128)S(1)} %get-tuple-element.61), channel_id=1, source_target_pairs={{0,4},{4,8},{8,12},{12,16},{16,20},{20,24},{24,28},{1,5},{5,9},{9,... | collective-permute-start | bytes 1179656 | tf_op jit(solution)/shard_map/ppermute | solution.py:19
  167.4 9.9 %collective-permute-start.10 = (f32[3,8,1,32,128]{4,3,2,1,0:T(8,128)S(1)}, f32[3,8,1,32,128]{4,3,2,1,0:T(8,128)S(1)}, u32[]{:S(2)}, u32[]{:S(2)}) collective-permute-start(f32[3,8,1,32,128]{4,3,2,1,0:T(8,128)S(1)} %get-tuple-element.58), channel_id=1, source_target_pairs={{4,0},{8,4},{12,8},{16,12},{20,16},{24,20},{28,24},{5,1},{9,5},{13... | collective-permute-start | bytes 1179656 | tf_op jit(solution)/shard_map/ppermute | solution.py:21
  168.8 13.1 %collective-permute-start.11 = (f32[3,8,1,32,128]{4,3,2,1,0:T(8,128)S(1)}, f32[3,8,1,32,128]{4,3,2,1,0:T(8,128)S(1)}, u32[]{:S(2)}, u32[]{:S(2)}) collective-permute-start(f32[3,8,1,32,128]{4,3,2,1,0:T(8,128)S(1)} %get-tuple-element.59), channel_id=1, source_target_pairs={{0,4},{4,8},{8,12},{12,16},{16,20},{20,24},{24,28},{1,5},{5,9},{9,... | collective-permute-start | bytes 1179656 | tf_op jit(solution)/shard_map/ppermute | solution.py:19
  210.0 4.0 collective-permute-start.12
  211.5 7.2 %collective-permute-start.13 = (f32[8,1,32,128]{3,2,1,0:T(8,128)S(1)}, f32[8,1,32,128]{3,2,1,0:T(8,128)S(1)}, u32[]{:S(2)}, u32[]{:S(2)}) collective-permute-start(f32[8,1,32,128]{3,2,1,0:T(8,128)S(1)} %get-tuple-element.85), channel_id=1, source_target_pairs={{4,0},{8,4},{12,8},{16,12},{20,16},{24,20},{28,24},{5,1},{9,5},{13... | collective-permute-start | bytes 393224 | tf_op jit(solution)/shard_map/ppermute | solution.py:21
  221.2 7.0 %collective-permute-start.14 = (f32[8,1,32,128]{3,2,1,0:T(8,128)S(1)}, f32[8,1,32,128]{3,2,1,0:T(8,128)S(1)}, u32[]{:S(2)}, u32[]{:S(2)}) collective-permute-start(f32[8,1,32,128]{3,2,1,0:T(8,128)S(1)} %get-tuple-element.82), channel_id=1, source_target_pairs={{4,0},{8,4},{12,8},{16,12},{20,16},{24,20},{28,24},{5,1},{9,5},{13... | collective-permute-start | bytes 393224 | tf_op jit(solution)/shard_map/ppermute | solution.py:21
  222.5 7.5 %collective-permute-start.15 = (f32[8,1,32,128]{3,2,1,0:T(8,128)S(1)}, f32[8,1,32,128]{3,2,1,0:T(8,128)S(1)}, u32[]{:S(2)}, u32[]{:S(2)}) collective-permute-start(f32[8,1,32,128]{3,2,1,0:T(8,128)S(1)} %get-tuple-element.83), channel_id=1, source_target_pairs={{0,4},{4,8},{8,12},{12,16},{16,20},{20,24},{24,28},{1,5},{5,9},{9,... | collective-permute-start | bytes 393224 | tf_op jit(solution)/shard_map/ppermute | solution.py:19
  272.5 6.9 %collective-permute-start.16 = (f32[8,1,32,128]{3,2,1,0:T(8,128)S(1)}, f32[8,1,32,128]{3,2,1,0:T(8,128)S(1)}, u32[]{:S(2)}, u32[]{:S(2)}) collective-permute-start(f32[8,1,32,128]{3,2,1,0:T(8,128)S(1)} %get-tuple-element.80), channel_id=1, source_target_pairs={{4,0},{8,4},{12,8},{16,12},{20,16},{24,20},{28,24},{5,1},{9,5},{13... | collective-permute-start | bytes 393224 | tf_op jit(solution)/shard_map/ppermute | solution.py:21
  273.8 7.1 %collective-permute-start.17 = (f32[8,1,32,128]{3,2,1,0:T(8,128)S(1)}, f32[8,1,32,128]{3,2,1,0:T(8,128)S(1)}, u32[]{:S(2)}, u32[]{:S(2)}) collective-permute-start(f32[8,1,32,128]{3,2,1,0:T(8,128)S(1)} %get-tuple-element.81), channel_id=1, source_target_pairs={{0,4},{4,8},{8,12},{12,16},{16,20},{20,24},{24,28},{1,5},{5,9},{9,... | collective-permute-start | bytes 393224 | tf_op jit(solution)/shard_map/ppermute | solution.py:19
  303.4 81.1 %copy-start = (f32[8,8,32,128]{3,2,1,0:T(8,128)}, f32[8,8,32,128]{3,2,1,0:T(8,128)S(1)}, u32[]{:S(2)}) copy-start(f32[8,8,32,128]{3,2,1,0:T(8,128)S(1)} %add_multiply_fusion.1) | copy-start | bytes 3145732
  303.5 8.1 %collective-permute-start.18 = (f32[8,1,32,128]{3,2,1,0:T(8,128)S(1)}, f32[8,1,32,128]{3,2,1,0:T(8,128)S(1)}, u32[]{:S(2)}, u32[]{:S(2)}) collective-permute-start(f32[8,1,32,128]{3,2,1,0:T(8,128)S(1)} %get-tuple-element.78), channel_id=1, source_target_pairs={{4,0},{8,4},{12,8},{16,12},{20,16},{24,20},{28,24},{5,1},{9,5},{13... | collective-permute-start | bytes 393224 | tf_op jit(solution)/shard_map/ppermute | solution.py:21
  304.8 8.8 %collective-permute-start.19 = (f32[8,1,32,128]{3,2,1,0:T(8,128)S(1)}, f32[8,1,32,128]{3,2,1,0:T(8,128)S(1)}, u32[]{:S(2)}, u32[]{:S(2)}) collective-permute-start(f32[8,1,32,128]{3,2,1,0:T(8,128)S(1)} %get-tuple-element.79), channel_id=1, source_target_pairs={{0,4},{4,8},{8,12},{12,16},{16,20},{20,24},{24,28},{1,5},{5,9},{9,... | collective-permute-start | bytes 393224 | tf_op jit(solution)/shard_map/ppermute | solution.py:19
  315.9 47.9 %copy-start.16 = (f32[8,32,128]{2,1,0:T(8,128)S(1)}, f32[8,32,128]{2,1,0:T(8,128)}, u32[]{:S(2)}) copy-start(f32[8,32,128]{2,1,0:T(8,128)} %copy-done.14) | copy-start | bytes 393220
  315.9 47.9 %copy-start.20 = (f32[8,32,128]{2,1,0:T(8,128)S(1)}, f32[8,32,128]{2,1,0:T(8,128)}, u32[]{:S(2)}) copy-start(f32[8,32,128]{2,1,0:T(8,128)} %copy-done.18) | copy-start | bytes 393220
  315.9 47.9 %copy-start.24 = (f32[8,32,128]{2,1,0:T(8,128)S(1)}, f32[8,32,128]{2,1,0:T(8,128)}, u32[]{:S(2)}) copy-start(f32[8,32,128]{2,1,0:T(8,128)} %copy-done.22) | copy-start | bytes 393220
  315.9 47.9 %copy-start.28 = (f32[8,32,128]{2,1,0:T(8,128)S(1)}, f32[8,32,128]{2,1,0:T(8,128)}, u32[]{:S(2)}) copy-start(f32[8,32,128]{2,1,0:T(8,128)} %copy-done.26) | copy-start | bytes 393220
  354.7 38.6 %copy-start.74 = (f32[8,32,128]{2,1,0:T(8,128)S(1)}, f32[8,32,128]{2,1,0:T(8,128)}, u32[]{:S(2)}) copy-start(f32[8,32,128]{2,1,0:T(8,128)} %get-tuple-element.107) | copy-start | bytes 393220
  354.8 7.0 %collective-permute-start.20 = (f32[8,1,32,128]{3,2,1,0:T(8,128)S(1)}, f32[8,1,32,128]{3,2,1,0:T(8,128)S(1)}, u32[]{:S(2)}, u32[]{:S(2)}) collective-permute-start(f32[8,1,32,128]{3,2,1,0:T(8,128)S(1)} %get-tuple-element.76), channel_id=1, source_target_pairs={{4,0},{8,4},{12,8},{16,12},{20,16},{24,20},{28,24},{5,1},{9,5},{13... | collective-permute-start | bytes 393224 | tf_op jit(solution)/shard_map/ppermute | solution.py:21
  356.2 7.6 %collective-permute-start.21 = (f32[8,1,32,128]{3,2,1,0:T(8,128)S(1)}, f32[8,1,32,128]{3,2,1,0:T(8,128)S(1)}, u32[]{:S(2)}, u32[]{:S(2)}) collective-permute-start(f32[8,1,32,128]{3,2,1,0:T(8,128)S(1)} %get-tuple-element.77), channel_id=1, source_target_pairs={{0,4},{4,8},{8,12},{12,16},{16,20},{20,24},{24,28},{1,5},{5,9},{9,... | collective-permute-start | bytes 393224 | tf_op jit(solution)/shard_map/ppermute | solution.py:19
  384.9 6.9 %collective-permute-start.22 = (f32[8,1,32,128]{3,2,1,0:T(8,128)S(1)}, f32[8,1,32,128]{3,2,1,0:T(8,128)S(1)}, u32[]{:S(2)}, u32[]{:S(2)}) collective-permute-start(f32[8,1,32,128]{3,2,1,0:T(8,128)S(1)} %get-tuple-element.74), channel_id=1, source_target_pairs={{4,0},{8,4},{12,8},{16,12},{20,16},{24,20},{28,24},{5,1},{9,5},{13... | collective-permute-start | bytes 393224 | tf_op jit(solution)/shard_map/ppermute | solution.py:21
  386.2 7.1 %collective-permute-start.23 = (f32[8,1,32,128]{3,2,1,0:T(8,128)S(1)}, f32[8,1,32,128]{3,2,1,0:T(8,128)S(1)}, u32[]{:S(2)}, u32[]{:S(2)}) collective-permute-start(f32[8,1,32,128]{3,2,1,0:T(8,128)S(1)} %get-tuple-element.75), channel_id=1, source_target_pairs={{0,4},{4,8},{8,12},{12,16},{16,20},{20,24},{24,28},{1,5},{5,9},{9,... | collective-permute-start | bytes 393224 | tf_op jit(solution)/shard_map/ppermute | solution.py:19
  395.0 13.7 %collective-permute-start.24 = (f32[3,8,1,32,128]{4,3,2,1,0:T(8,128)S(1)}, f32[3,8,1,32,128]{4,3,2,1,0:T(8,128)S(1)}, u32[]{:S(2)}, u32[]{:S(2)}) collective-permute-start(f32[3,8,1,32,128]{4,3,2,1,0:T(8,128)S(1)} %get-tuple-element.56), channel_id=1, source_target_pairs={{4,0},{8,4},{12,8},{16,12},{20,16},{24,20},{28,24},{5,1},{9,5},{13... | collective-permute-start | bytes 1179656 | tf_op jit(solution)/shard_map/ppermute | solution.py:21
  396.4 20.8 %collective-permute-start.25 = (f32[3,8,1,32,128]{4,3,2,1,0:T(8,128)S(1)}, f32[3,8,1,32,128]{4,3,2,1,0:T(8,128)S(1)}, u32[]{:S(2)}, u32[]{:S(2)}) collective-permute-start(f32[3,8,1,32,128]{4,3,2,1,0:T(8,128)S(1)} %get-tuple-element.57), channel_id=1, source_target_pairs={{0,4},{4,8},{8,12},{12,16},{16,20},{20,24},{24,28},{1,5},{5,9},{9,... | collective-permute-start | bytes 1179656 | tf_op jit(solution)/shard_map/ppermute | solution.py:19
  466.5 9.7 %collective-permute-start.26 = (f32[3,8,1,32,128]{4,3,2,1,0:T(8,128)S(1)}, f32[3,8,1,32,128]{4,3,2,1,0:T(8,128)S(1)}, u32[]{:S(2)}, u32[]{:S(2)}) collective-permute-start(f32[3,8,1,32,128]{4,3,2,1,0:T(8,128)S(1)} %get-tuple-element.54), channel_id=1, source_target_pairs={{4,0},{8,4},{12,8},{16,12},{20,16},{24,20},{28,24},{5,1},{9,5},{13... | collective-permute-start | bytes 1179656 | tf_op jit(solution)/shard_map/ppermute | solution.py:21
  467.8 13.0 %collective-permute-start.27 = (f32[3,8,1,32,128]{4,3,2,1,0:T(8,128)S(1)}, f32[3,8,1,32,128]{4,3,2,1,0:T(8,128)S(1)}, u32[]{:S(2)}, u32[]{:S(2)}) collective-permute-start(f32[3,8,1,32,128]{4,3,2,1,0:T(8,128)S(1)} %get-tuple-element.55), channel_id=1, source_target_pairs={{0,4},{4,8},{8,12},{12,16},{16,20},{20,24},{24,28},{1,5},{5,9},{9,... | collective-permute-start | bytes 1179656 | tf_op jit(solution)/shard_map/ppermute | solution.py:19
  508.1 4.0 collective-permute-start.28
  509.6 7.1 %collective-permute-start.29 = (f32[8,1,32,128]{3,2,1,0:T(8,128)S(1)}, f32[8,1,32,128]{3,2,1,0:T(8,128)S(1)}, u32[]{:S(2)}, u32[]{:S(2)}) collective-permute-start(f32[8,1,32,128]{3,2,1,0:T(8,128)S(1)} %get-tuple-element.73), channel_id=1, source_target_pairs={{4,0},{8,4},{12,8},{16,12},{20,16},{24,20},{28,24},{5,1},{9,5},{13... | collective-permute-start | bytes 393224 | tf_op jit(solution)/shard_map/ppermute | solution.py:21
  519.1 6.9 %collective-permute-start.30 = (f32[8,1,32,128]{3,2,1,0:T(8,128)S(1)}, f32[8,1,32,128]{3,2,1,0:T(8,128)S(1)}, u32[]{:S(2)}, u32[]{:S(2)}) collective-permute-start(f32[8,1,32,128]{3,2,1,0:T(8,128)S(1)} %get-tuple-element.70), channel_id=1, source_target_pairs={{4,0},{8,4},{12,8},{16,12},{20,16},{24,20},{28,24},{5,1},{9,5},{13... | collective-permute-start | bytes 393224 | tf_op jit(solution)/shard_map/ppermute | solution.py:21
  520.4 7.1 %collective-permute-start.31 = (f32[8,1,32,128]{3,2,1,0:T(8,128)S(1)}, f32[8,1,32,128]{3,2,1,0:T(8,128)S(1)}, u32[]{:S(2)}, u32[]{:S(2)}) collective-permute-start(f32[8,1,32,128]{3,2,1,0:T(8,128)S(1)} %get-tuple-element.71), channel_id=1, source_target_pairs={{0,4},{4,8},{8,12},{12,16},{16,20},{20,24},{24,28},{1,5},{5,9},{9,... | collective-permute-start | bytes 393224 | tf_op jit(solution)/shard_map/ppermute | solution.py:19
  551.3 48.3 %copy-start.40 = (f32[8,32,128]{2,1,0:T(8,128)S(1)}, f32[8,32,128]{2,1,0:T(8,128)}, u32[]{:S(2)}) copy-start(f32[8,32,128]{2,1,0:T(8,128)} %param.10) | copy-start | bytes 393220
  570.3 6.9 %collective-permute-start.32 = (f32[8,1,32,128]{3,2,1,0:T(8,128)S(1)}, f32[8,1,32,128]{3,2,1,0:T(8,128)S(1)}, u32[]{:S(2)}, u32[]{:S(2)}) collective-permute-start(f32[8,1,32,128]{3,2,1,0:T(8,128)S(1)} %get-tuple-element.68), channel_id=1, source_target_pairs={{4,0},{8,4},{12,8},{16,12},{20,16},{24,20},{28,24},{5,1},{9,5},{13... | collective-permute-start | bytes 393224 | tf_op jit(solution)/shard_map/ppermute | solution.py:21
  571.6 7.2 %collective-permute-start.33 = (f32[8,1,32,128]{3,2,1,0:T(8,128)S(1)}, f32[8,1,32,128]{3,2,1,0:T(8,128)S(1)}, u32[]{:S(2)}, u32[]{:S(2)}) collective-permute-start(f32[8,1,32,128]{3,2,1,0:T(8,128)S(1)} %get-tuple-element.69), channel_id=1, source_target_pairs={{0,4},{4,8},{8,12},{12,16},{16,20},{20,24},{24,28},{1,5},{5,9},{9,... | collective-permute-start | bytes 393224 | tf_op jit(solution)/shard_map/ppermute | solution.py:19
  (75 other events, 1011.6 us)
where the time goes:
time: 674 us; the launch traced here: 663 us
  blocking collectives  398 us (59%)
  starting transfers between devices  97.3 us (14%)
  waiting for transfers between devices  81.6 us (12%)
  other arithmetic  79.2 us (12%)
    psum x18, blocking collectives, inner(): return lax.psum(summed, 'tile')  344 us
    ppermute x17, starting transfers between devices, extended(): lax.ppermute(tail, axis, [(i, (i + 1) % count) for i in range(ends)])  74.3 us
    ppermute x17, waiting for transfers between devices, extended(): lax.ppermute(tail, axis, [(i, (i + 1) % count) for i in range(ends)])  43.2 us
    ppermute x17, waiting for transfers between devices, extended(): lax.ppermute(head, axis, [((i + 1) % count, i) for i in range(ends)])  38.3 us
    psum x1, blocking collectives, body(): gram_whole = lax.psum(gram_local, ('tile', 'dir'))  36.9 us
    ppermute x17, starting transfers between devices, extended(): lax.ppermute(head, axis, [((i + 1) % count, i) for i in range(ends)])  23 us
    reduce_sum x6, other arithmetic, inner(): summed = jnp.sum(summed, axis=0)  21.1 us
    all_to_all x1, blocking collectives, body(): lax.all_to_all(hess_block, 'dir', split_axis=2, concat_axis=0, tiled=True)  17.3 us
  transfers between devices with their start and end apart: 34, of which 32 were waited for; matrix products, arithmetic and copies ran while one was open for 0% of the time, Pallas kernels for 0%

commit v1 on v0

--- a/solution.py
+++ b/solution.py
@@ -1,6 +1,10 @@
+import functools
+
 import jax
 import jax.numpy as jnp
 from jax import lax
+from jax.experimental import pallas as pl
+from jax.experimental.pallas import tpu as pltpu
 from jax.sharding import PartitionSpec as P
 
 NCLASS = 8
@@ -109,7 +113,7 @@
     return iterate
 
 
-def body(
+def halo_body(
     probes,
     base_sens,
     obs_weight,
@@ -182,6 +186,699 @@
     r_factor = jnp.linalg.cholesky(gram_whole).T
     return (hess_block, r_factor)
 
+MESH = pl.DeviceIdType.MESH
+SUBL = 8
+LANES = 128
+PAD = 8
+
+
+def whole_sum(acc):
+    return jnp.sum(jnp.sum(acc, axis=1, keepdims=True), axis=0, keepdims=True)
+
+
+def kernel(
+    dims,
+    tables,
+    src_in,
+    pm_in,
+    obs_in,
+    bs_in,
+    adj,
+    r_out,
+    src_all,
+    pm_all,
+    obs_all,
+    out_all,
+    gat,
+    ycol,
+    part_dir,
+    part_tile,
+    perm_f,
+    shear_f,
+    diag_f,
+    stab_f,
+    hb_f,
+    pcs,
+    pcx,
+    pcy,
+    pcz,
+    ecs,
+    ecx,
+    ecy,
+    ecz,
+    r0,
+    r1,
+    pb,
+    wb,
+    tb,
+    eb,
+    fb,
+    we,
+    pm_send,
+    pm_recv,
+    fw_send,
+    fw_recv,
+    src_send,
+    src_recv,
+    obs_send,
+    obs_recv,
+    ret_send,
+    ret_recv,
+    y_send,
+    y_recv,
+    g_send,
+    g_recv,
+    t_send,
+    t_recv,
+    own_sem,
+):
+    nt, nd, nx, ny, cells = dims
+    rows = nx * ny
+    half = rows // 2
+    quarter = rows // nd
+    pitch = rows + PAD
+    pm_pitch = 2 * rows + PAD
+    gpitch = quarter + PAD
+    me = lax.axis_index("tile")
+    q = lax.axis_index("dir")
+    core = lax.rem(q, 2)
+    partner = q + 1 - 2 * core
+
+    def span(start, size):
+        return pl.ds(pl.multiple_of(start, 8), size)
+
+    def ahead(k):
+        return lax.rem(me + k, nt)
+
+    def behind(k):
+        return lax.rem(me + nt - k, nt)
+
+    barrier = pltpu.get_barrier_semaphore()
+    for k in range(1, nt):
+        pl.semaphore_signal(barrier, inc=1, device_id={"tile": ahead(k)}, device_id_type=MESH)
+    for m in range(1, nd):
+        pl.semaphore_signal(
+            barrier, inc=1, device_id={"dir": lax.rem(q + m, nd)}, device_id_type=MESH
+        )
+    pl.semaphore_wait(barrier, nt + nd - 2)
+
+    def remote(src, dst, send, recv, axis, to):
+        return pltpu.make_async_remote_copy(
+            src_ref=src,
+            dst_ref=dst,
+            send_sem=send,
+            recv_sem=recv,
+            device_id={axis: to},
+            device_id_type=MESH,
+        )
+
+    def pm_copy(k, owner, to):
+        return remote(
+            pm_in.at[span(core * rows, rows)],
+            pm_all.at[span(owner * pm_pitch + core * rows, rows)],
+            pm_send.at[k],
+            pm_recv.at[k],
+            "tile",
+            to,
+        )
+
+    def src_copy(k, owner, to):
+        return remote(
+            src_in.at[span(to * rows, rows)],
+            src_all.at[span(owner * pitch, rows)],
+            src_send.at[k],
+            src_recv.at[k],
+            "tile",
+            to,
+        )
+
+    def obs_copy(k, owner, to):
+        return remote(
+            obs_in, obs_all.at[span(owner * pitch, rows)], obs_send.at[k], obs_recv.at[k], "tile", to
+        )
+
+    def fw_copy(k, which):
+        owner = behind(k)
+        place = pm_all.at[span(owner * pm_pitch + which * rows, rows)]
+        source = pm_in.at[span(which * rows, rows)] if k == 0 else place
+        return remote(source, place, fw_send.at[k], fw_recv.at[k], "dir", partner)
+
+    for k in range(1, nt):
+        pm_copy(k, me, ahead(k)).start()
+    for k in range(1, nt):
+        src_copy(k, me, ahead(k)).start()
+    own = [
+        pltpu.make_async_copy(
+            pm_in.at[span(core * rows, rows)],
+            pm_all.at[span(me * pm_pitch + core * rows, rows)],
+            own_sem.at[0],
+        ),
+        pltpu.make_async_copy(
+            src_in.at[span(me * rows, rows)], src_all.at[span(me * pitch, rows)], own_sem.at[1]
+        ),
+        pltpu.make_async_copy(obs_in, obs_all.at[span(me * pitch, rows)], own_sem.at[2]),
+    ]
+    for copy in own:
+        copy.start()
+    fw_copy(0, core).start()
+    for k in range(1, nt):
+        pm_copy(k, behind(k), behind(k)).wait_recv()
+        fw_copy(k, core).start()
+    own[0].wait()
+    for k in range(nt):
+        fw_copy(k, 1 - core).wait_recv()
+
+    sub = lax.broadcasted_iota(jnp.int32, (SUBL, LANES), 0)
+    lane = lax.broadcasted_iota(jnp.int32, (SUBL, LANES), 1)
+    sub_lo, sub_hi = sub > 0, sub < SUBL - 1
+    lane_lo, lane_hi = lane > 0, lane < LANES - 1
+    zero = jnp.zeros((SUBL, LANES), jnp.float32)
+
+    def down(v):
+        return jnp.where(sub_lo, pltpu.roll(v, 1, 0), 0.0)
+
+    def up(v):
+        return jnp.where(sub_hi, pltpu.roll(v, SUBL - 1, 0), 0.0)
+
+    def next_z(v):
+        return pltpu.roll(v, LANES - 1, 1)
+
+    def prev_z(v):
+        return pltpu.roll(v, 1, 1)
+
+    def halo(field):
+        for y in range(ny):
+            field[0, y] = down(field[nx, y])
+            field[nx + 1, y] = up(field[1, y])
+
+    def planes(step, init):
+        return lax.fori_loop(0, nx, step, init)
+
+    half_planes = nx // 2
+
+    def lookup(x, _):
+        block = x // half_planes
+        inside = x - block * half_planes
+        base = block * rows + inside * ny
+        for y in range(ny):
+            perm_f[x + 1, y] = pm_all[pl.ds(base + y, SUBL, stride=pm_pitch), :]
+            mat = pm_all[pl.ds(base + half + y, SUBL, stride=pm_pitch), :]
+            storage, alpha, bulk, shear = zero, zero, zero, zero
+            for c in range(NCLASS):
+                hit = mat == float(c)
+                storage = jnp.where(hit, tables[0, c], storage)
+                alpha = jnp.where(hit, tables[1, c], alpha)
+                bulk = jnp.where(hit, tables[2, c], bulk)
+                shear = jnp.where(hit, tables[3, c], shear)
+            stab = alpha * alpha / bulk
+            stab_f[x, y] = stab
+            diag_f[x, y] = storage + stab
+            hb_f[x, y] = 0.5 * alpha
+            shear_f[x + 1, y] = shear
+        return 0
+
+    planes(lookup, 0)
+
+    for coef, cs, cx, cy, cz, diag in (
+        (perm_f, pcs, pcx, pcy, pcz, diag_f),
+        (shear_f, ecs, ecx, ecy, ecz, None),
+    ):
+        halo(coef)
+
+        def faces(x, _):
+            for y in range(ny):
+                mid = coef[x + 1, y]
+                after = coef[x + 2, y]
+                total = coef[x, y] + after
+                nz_val = jnp.where(lane_hi, next_z(mid), 0.0)
+                total = total + nz_val + jnp.where(lane_lo, prev_z(mid), 0.0)
+                if y > 0:
+                    total = total + coef[x + 1, y - 1]
+                if y < ny - 1:
+                    right = coef[x + 1, y + 1]
+                    total = total + right
+                    cy[x, y] = 0.5 * (mid + right)
+                else:
+                    cy[x, y] = zero
+                cz[x, y] = jnp.where(lane_hi, 0.5 * (mid + nz_val), 0.0)
+                face = 0.5 * (mid + after)
+                cx[x + 1, y] = jnp.where(jnp.logical_or(x < nx - 1, sub_hi), face, 0.0)
+                value = 3.0 * mid + 0.5 * total
+                if diag is not None:
+                    value = value + diag[x, y]
+                cs[x, y] = value
+            return 0
+
+        planes(faces, 0)
+        for y in range(ny):
+            cx[0, y] = down(cx[nx, y])
+
+    def stencil(fields, index, coefs, x, emit, carry):
+        cs, cx, cy, cz = coefs
+        count = len(index)
+        before = [None] * count
+        here = [fields(i, x + 1, 0) for i in range(count)]
+        cy_before = None
+        for y in range(ny):
+            s, c_next, c_prev = cs[x, y], cx[x + 1, y], cx[x, y]
+            c_y, c_z = cy[x, y], cz[x, y]
+            images = []
+            centers = []
+            for i in range(count):
+                v = here[i]
+                out = s * v - c_next * fields(i, x + 2, y) - c_prev * fields(i, x, y)
+                out = out - (c_z * next_z(v) + prev_z(c_z * v))
+                if y > 0:
+                    out = out - cy_before * before[i]
+                after = None
+                if y < ny - 1:
+                    after = fields(i, x + 1, y + 1)
+                    out = out - c_y * after
+                images.append(out)
+                centers.append(v)
+                before[i], here[i] = v, after
+            cy_before = c_y
+            carry = emit(y, centers, images, carry)
+        return carry
+
+    def single(field):
+        return lambda i, x, y: field[x, y]
+
+    def triple(field):
+        return lambda i, x, y: field[i, x, y]
+
+    press = (pcs, pcx, pcy, pcz)
+    elast = (ecs, ecx, ecy, ecz)
+
+    def first_apply(fields, index, coefs, store):
+        def step(x, carry):
+            def emit(y, centers, images, acc):
+                a, b = acc
+                for i in index:
+                    store(i, x, y, images[i])
+                    a = a + centers[i] * centers[i]
+                    b = b + centers[i] * images[i]
+                return a, b
+
+            return stencil(fields, index, coefs, x, emit, carry)
+
+        a, b = planes(step, (zero, zero))
+        return whole_sum(a), whole_sum(b)
+
+    def second_apply(fields, olds, oldw, index, coefs, beta, store):
+        def step(x, carry):
+            def emit(y, centers, images, acc):
+                for i in index:
+                    w = images[i] + beta * oldw(i, x, y)
+                    d = centers[i] + beta * olds(i, x + 1, y)
+                    acc = acc + d * w
+                    if store is not None:
+                        store(i, x, y, w)
+                return acc
+
+            return stencil(fields, index, coefs, x, emit, carry)
+
+        return whole_sum(planes(step, zero))
+
+    def wb_store(i, x, y, value):
+        wb[x, y] = value
+
+    def we_store(i, x, y, value):
+        we[i, x, y] = value
+
+    def press_steps(keep):
+        halo(r0)
+        rr, rw = first_apply(single(r0), (0,), press, wb_store)
+        a0 = rr / rw
+
+        def residual(x, acc):
+            for y in range(ny):
+                v = r0[x + 1, y] - a0 * wb[x, y]
+                r1[x + 1, y] = v
+                acc = acc + v * v
+            return acc
+
+        rr1 = whole_sum(planes(residual, zero))
+        beta = rr1 / rr
+        halo(r1)
+        dw = second_apply(
+            single(r1),
+            single(r0),
+            lambda i, x, y: wb[x, y],
+            (0,),
+            press,
+            beta,
+            wb_store if keep else None,
+        )
+        return a0, rr1 / dw, beta
+
+    for k in range(1, nt):
+        src_copy(k, behind(k), behind(k)).wait_recv()
+    own[1].wait()
+    for k in range(1, nt):
+        obs_copy(k, me, ahead(k)).start()
+
+    def take_source(x, _):
+        for y in range(ny):
+            r0[x + 1, y] = src_all[pl.ds(x * ny + y, SUBL, stride=pitch), :]
+        return 0
+
+    planes(take_source, 0)
+
+    def solve(turn, _):
+        a0, a1, beta = press_steps(True)
+        c0 = a0 + a1 * beta
+
+        def first_press(x, _):
+            for y in range(ny):
+                old = r1[x + 1, y]
+                p = c0 * r0[x + 1, y] + a1 * old
+                pb[x + 1, y] = p
+                tb[x, y] = old - a1 * wb[x, y] + stab_f[x, y] * p
+            return 0
+
+        planes(first_press, 0)
+        halo(pb)
+
+        def grad(x, _):
+            for y in range(ny):
+                b = hb_f[x, y]
+                v = pb[x + 1, y]
+                eb[0, x + 1, y] = b * (pb[x + 2, y] - pb[x, y])
+                hi = pb[x + 1, y + 1] if y < ny - 1 else zero
+                lo = pb[x + 1, y - 1] if y > 0 else zero
+                eb[1, x + 1, y] = b * (hi - lo)
+                eb[2, x + 1, y] = b * (
+                    jnp.where(lane_hi, next_z(v), 0.0) - jnp.where(lane_lo, prev_z(v), 0.0)
+                )
+            return 0
+
+        planes(grad, 0)
+        for i in range(3):
+            halo(eb.at[i])
+        comps = (0, 1, 2)
+        rr, rw = first_apply(triple(eb), comps, elast, we_store)
+        b0 = rr / rw
+
+        def residual(x, acc):
+            for y in range(ny):
+                for i in comps:
+                    v = eb[i, x + 1, y] - b0 * we[i, x, y]
+                    fb[i, x + 1, y] = v
+                    acc = acc + v * v
+            return acc
+
+        rr1 = whole_sum(planes(residual, zero))
+        beta_e = rr1 / rr
+        for i in range(3):
+            halo(fb.at[i])
+        dw = second_apply(
+            triple(fb), triple(eb), lambda i, x, y: we[i, x, y], comps, elast, beta_e, None
+        )
+        b1 = rr1 / dw
+        e0 = b0 + b1 * beta_e
+
+        def weigh(x, _):
+            for y in range(ny):
+                b = hb_f[x, y]
+                for i in comps:
+                    eb[i, x + 1, y] = b * (e0 * eb[i, x + 1, y] + b1 * fb[i, x + 1, y])
+            return 0
+
+        planes(weigh, 0)
+        halo(eb.at[0])
+
+        def next_source(x, _):
+            for y in range(ny):
+                total = tb[x, y] - (eb[0, x, y] - eb[0, x + 2, y])
+                if y > 0:
+                    total = total - eb[1, x + 1, y - 1]
+                if y < ny - 1:
+                    total = total + eb[1, x + 1, y + 1]
+                w = eb[2, x + 1, y]
+                total = total - (
+                    jnp.where(lane_lo, prev_z(w), 0.0) - jnp.where(lane_hi, next_z(w), 0.0)
+                )
+                r0[x + 1, y] = total
+            return 0
+
+        planes(next_source, 0)
+        a0, a1, beta = press_steps(False)
+        c0 = a0 + a1 * beta
+
+        @pl.when(turn == 0)
+        def _():
+            for k in range(1, nt):
+                obs_copy(k, behind(k), behind(k)).wait_recv()
+            own[2].wait()
+
+            def last_press(x, _):
+                for y in range(ny):
+                    p = pb[x + 1, y] + c0 * r0[x + 1, y] + a1 * r1[x + 1, y]
+                    r0[x + 1, y] = p * obs_all[pl.ds(x * ny + y, SUBL, stride=pitch), :]
+                return 0
+
+            planes(last_press, 0)
+
+        @pl.when(turn == 1)
+        def _():
+            def last_press(x, _):
+                for y in range(ny):
+                    p = pb[x + 1, y] + c0 * r0[x + 1, y] + a1 * r1[x + 1, y]
+                    out_all[pl.ds(x * ny + y, SUBL, stride=pitch), :] = p
+                return 0
+
+            planes(last_press, 0)
+
+        return 0
+
+    lax.fori_loop(0, 2, solve, 0)
+
+    order = [nd // 2] + [m for m in range(1, nd) if m != nd // 2] + [0]
+
+    def ret_copy(m, k, owner, to):
+        chunk = lax.rem(q + m, nd)
+        return remote(
+            out_all.at[span(to * pitch + chunk * quarter, quarter)],
+            adj.at[span(owner * rows + chunk * quarter, quarter)],
+            ret_send.at[m, k],
+            ret_recv.at[m, k],
+            "tile",
+            to,
+        )
+
+    def own_copy(m):
+        chunk = lax.rem(q + m, nd)
+        return pltpu.make_async_copy(
+            out_all.at[span(me * pitch + chunk * quarter, quarter)],
+            adj.at[span(me * rows + chunk * quarter, quarter)],
+            own_sem.at[m],
+        )
+
+    def y_copy(m, k, group, chunk, to):
+        owner = behind(k)
+        return remote(
+            adj.at[span(owner * rows + chunk * quarter, quarter)],
+            gat.at[span((group * nt + owner) * gpitch, quarter)],
+            y_send.at[m, k],
+            y_recv.at[m, k],
+            "dir",
+            to,
+        )
+
+    for m in order:
+        own_copy(m).start()
+        for k in range(1, nt):
+            ret_copy(m, k, me, ahead(k)).start()
+    for m in order:
+        to = lax.rem(q + m, nd)
+        for k in range(nt):
+            if k == 0:
+                own_copy(m).wait()
+            else:
+                ret_copy(m, k, behind(k), behind(k)).wait_recv()
+            if m > 0:
+                y_copy(m, k, q, to, to).start()
+
+    def columns(source, stride, base, group):
+        def fill(r, _):
+            value = source[pl.ds(base + r, SUBL, stride=stride), :]
+            scale = bs_in[pl.ds(q * quarter + r, 1), :]
+            ycol[span(group * SUBL, SUBL), pl.ds(pl.multiple_of(r * LANES, LANES), LANES)] = (
+                value * scale
+            )
+            return 0
+
+        lax.fori_loop(0, quarter, fill, 0, unroll=8)
+
+    columns(adj, rows, q * quarter, q)
+    for m in order[:-1]:
+        group = lax.rem(q + nd - m, nd)
+        for k in range(nt):
+            y_copy(m, k, group, q, group).wait_recv()
+        columns(gat, gpitch, group * nt * gpitch, group)
+
+    nall = nd * nt
+    gram = lax.dot_general(
+        ycol[...],
+        ycol[...],
+        (((1,), (1,)), ((), ())),
+        precision=lax.Precision.HIGHEST,
+        preferred_element_type=jnp.float32,
+    )
+
+    def gather_sum(slots, place, send, recv, axis, count):
+        def copy(k, owner, to):
+            return remote(slots.at[owner], slots.at[owner], send.at[k], recv.at[k], axis, to)
+
+        for k in range(1, count):
+            copy(k, place, lax.rem(place + k, count)).start()
+        for k in range(1, count):
+            owner = lax.rem(place + count - k, count)
+            copy(k, owner, owner).wait_recv()
+        total = slots[0]
+        for s in range(1, count):
+            total = total + slots[s]
+        for k in range(1, count):
+            copy(k, place, lax.rem(place + k, count)).wait_send()
+        return total
+
+    part_dir[q] = jnp.zeros((nall, LANES), jnp.float32)
+    part_dir[q, :, 0:nall] = gram
+    part_tile[me] = gather_sum(part_dir, q, g_send, g_recv, "dir", nd)
+    mat = gather_sum(part_tile, me, t_send, t_recv, "tile", nt) / cells
+
+    lanes_all = lax.broadcasted_iota(jnp.int32, (1, LANES), 1)
+    for j in range(nall):
+        root = jnp.sqrt(mat[j : j + 1, j : j + 1])
+        row = mat[j : j + 1, :] / root
+        r_out[j : j + 1, :] = jnp.where(lanes_all >= j, row, 0.0)[:, 0:nall]
+        mat = mat - (mat[:, j : j + 1] / root) * row
+
+    for k in range(1, nt):
+        pm_copy(k, me, ahead(k)).wait_send()
+        src_copy(k, me, ahead(k)).wait_send()
+        obs_copy(k, me, ahead(k)).wait_send()
+        for m in order:
+            ret_copy(m, k, me, ahead(k)).wait_send()
+    for k in range(nt):
+        fw_copy(k, core).wait_send()
+        for m in order[:-1]:
+            to = lax.rem(q + m, nd)
+            y_copy(m, k, q, to, to).wait_send()
+
+
+def local_body(
+    probes,
+    base_sens,
+    obs_weight,
+    perm,
+    material,
+    class_storage,
+    class_alpha,
+    class_bulk,
+    class_shear,
+):
+    nt, nd = lax.axis_size("tile"), lax.axis_size("dir")
+    count, nx, ny, nz = probes.shape
+    rows = nx * ny
+    tables = jnp.stack([class_storage, class_alpha, class_bulk, class_shear])
+    source = (base_sens * probes).reshape(count * rows, nz)
+    coefs = jnp.stack(
+        [
+            perm.reshape(2, rows // 2, nz),
+            material.astype(jnp.float32).reshape(2, rows // 2, nz),
+        ],
+        axis=1,
+    ).reshape(2 * rows, nz)
+    nall = nd * count
+    quarter = rows // nd
+    vmem = pl.BlockSpec(memory_space=pltpu.VMEM)
+    f32 = jnp.float32
+
+    def rowbuf(n):
+        return pltpu.VMEM((n, nz), f32)
+
+    def field(n):
+        return pltpu.VMEM((n, ny, SUBL, LANES), f32)
+
+    def fields(n):
+        return pltpu.VMEM((3, n, ny, SUBL, LANES), f32)
+
+    sems = pltpu.SemaphoreType.DMA
+    inner_f, outer_f = field(nx), field(nx + 2)
+    scratch = [
+        rowbuf(nt * (rows + PAD)),
+        rowbuf(nt * (2 * rows + PAD)),
+        rowbuf(nt * (rows + PAD)),
+        rowbuf(nt * (rows + PAD)),
+        rowbuf(nall * (quarter + PAD)),
+        pltpu.VMEM((nall, quarter * nz), f32),
+        pltpu.VMEM((nd, nall, LANES), f32),
+        pltpu.VMEM((nt, nall, LANES), f32),
+        outer_f,
+        outer_f,
+        inner_f,
+        inner_f,
+        inner_f,
+        inner_f,
+        field(nx + 1),
+        inner_f,
+        inner_f,
+        inner_f,
+        field(nx + 1),
+        inner_f,
+        inner_f,
+        outer_f,
+        outer_f,
+        outer_f,
+        inner_f,
+        inner_f,
+        fields(nx + 2),
+        fields(nx + 2),
+        fields(nx),
+        sems((nt,)),
+        sems((nt,)),
+        sems((nt,)),
+        sems((nt,)),
+        sems((nt,)),
+        sems((nt,)),
+        sems((nt,)),
+        sems((nt,)),
+        sems((nd, nt)),
+        sems((nd, nt)),
+        sems((nd, nt)),
+        sems((nd, nt)),
+        sems((nd,)),
+        sems((nd,)),
+        sems((nt,)),
+        sems((nt,)),
+        sems((max(nd, 3),)),
+    ]
+    adjoint, r_factor = pl.pallas_call(
+        functools.partial(kernel, (nt, nd, nx, ny, float(nt * rows * nz))),
+        out_shape=(
+            jax.ShapeDtypeStruct((count * rows, nz), f32),
+            jax.ShapeDtypeStruct((nall, nall), f32),
+        ),
+        in_specs=[pl.BlockSpec(memory_space=pltpu.SMEM)] + [vmem] * 4,
+        out_specs=(vmem, vmem),
+        scratch_shapes=scratch,
+        compiler_params=pltpu.CompilerParams(
+            collective_id=0, has_side_effects=True, vmem_limit_bytes=60 * 1024 * 1024
+        ),
+    )(tables, source, coefs, obs_weight.reshape(rows, nz), base_sens.reshape(rows, nz))
+    return (base_sens * adjoint.reshape(probes.shape), r_factor)
+
+
+def body(probes, *others):
+    nt, nd = lax.axis_size("tile"), lax.axis_size("dir")
+    count, nx, ny, nz = probes.shape
+    fits = nt == SUBL and count == nt and nz == LANES and nd % 2 == 0 and nx % 2 == 0
+    fits = fits and ny % 8 == 0 and (nx * ny) % (8 * nd) == 0 and nd * nt <= LANES
+    fits = fits and nx * ny * nz <= 32768
+    return (local_body if fits else halo_body)(probes, *others)
+
 
 def solution(mesh):
     placed = (

time: 674 us -> 139 us (0.21); the launches traced: 663 us -> 138 us
  blocking collectives: 398 us -> 0 us
  Pallas kernels: 0 us -> 129 us
  starting transfers between devices: 97.3 us -> 0 us
  waiting for transfers between devices: 81.6 us -> 0 us
  other arithmetic: 79.2 us -> 6.92 us
    psum x19 -> x0, blocking collectives: 381 us -> none  [the longest x18 344 us: inner(): return lax.psum(summed, 'tile')]
    pallas_call x0 -> x1, Pallas kernels: none -> 129 us  [local_body(): pl.pallas_call(functools.partial(kernel, (nt, nd, nx, ny, float(nt * rows...]
    ppermute x34 -> x0, starting transfers between devices: 97.3 us -> none  [the longest x17 74.3 us: extended(): lax.ppermute(tail, axis, [(i, (i + 1) % count) for i in range(ends)])]
    ppermute x34 -> x0, waiting for transfers between devices: 81.6 us -> none  [the longest x17 43.2 us: extended(): lax.ppermute(tail, axis, [(i, (i + 1) % count) for i in range(ends)])]
    reduce_sum x19 -> x0, other arithmetic: 38.2 us -> none  [the longest x6 21.1 us: inner(): summed = jnp.sum(summed, axis=0)]
    add x10 -> x0, other arithmetic: 17.8 us -> none  [the longest x6 11.7 us: conj_grad(): direction = residual + spread(norm_next / norm_now) * direction]
    all_to_all x1 -> x0, blocking collectives: 17.3 us -> none  [body(): lax.all_to_all(hess_block, 'dir', split_axis=2, concat_axis=0, tiled=True)]
  transfers between devices with their start and end apart: 34 -> 0, of which waited for: 32 -> 0; matrix products, arithmetic and copies ran while one was open for 0% -> 0% of each run, Pallas kernels for 0% -> 0%
where the time goes in v1:
time: 139 us; the launch traced here: 138 us
  Pallas kernels  129 us (93%)
  other arithmetic  6.92 us (5%)
  local copies, waits for them, and re-layouts  1.51 us (1%)
    pallas_call x1, Pallas kernels, local_body(): pl.pallas_call(functools.partial(kernel, (nt, nd, nx, ny, float(nt * rows...  129 us

profile of v1, /device:TPU:0, one launch (start us, length us, event | category | flops | bytes accessed | tf_op | source)
XLA Modules:
  0.0 138.5 jit_solution(4254843868772058984)
XLA Ops:
  0.6 0.0 copy-start.7
  0.6 0.0 copy-start.4
  0.7 0.0 copy-start.5
  0.7 0.0 copy-start.6
  0.7 0.6 copy-done.7
  1.3 0.0 copy-done.4
  1.3 0.0 copy-done.5
  1.3 0.0 copy-done.6
  1.3 0.6 pad_maximum_fusion.1.tables
  1.9 0.0 copy-start.2
  1.9 0.9 convert_element_type.3
  2.9 0.0 copy-done.2
  2.9 0.0 copy-start
  2.9 0.7 pad_maximum_fusion
  3.6 0.2 copy-done
  3.8 2.3 %broadcast_multiply_fusion.1 = f32[8,8,32,128]{3,2,1,0:T(8,128)} fusion(f32[8,8,32,128]{3,2,1,0:T(8,128)} %param.9, f32[8,32,128]{2,1,0:T(8,128)S(1)} %copy-done), kind=kLoop, calls=%fused_computation.1 | loop fusion | flops 262144 | bytes 2228224 | tf_op jit(solution)/shard_map/mul | solution.py:786
  6.2 0.0 copy-start.1
  6.2 129.3 %shard_map.104 = (f32[2048,128]{1,0:T(8,128)}, f32[32,32]{1,0:T(8,128)}) custom-call(f32[4,8]{1,0:T(4,128)} %pad_maximum_fusion.1.tables, f32[2048,128]{1,0:T(8,128)} %bitcast.15, f32[512,128]{1,0:T(8,128)} %bitcast.18, f32[256,128]{1,0:T(8,128)} %bitcast.20, f32[256,128]{1,0:T(8,128)} %bitcast.16), custom_call_target="tpu_custom_call" | custom-call | tf_op jit(solution)/shard_map/pallas_call | solution.py:858
  135.5 0.0 copy-done.1
  135.5 0.0 copy-start.3
  135.5 2.3 %broadcast_multiply_fusion = f32[8,8,32,128]{3,2,1,0:T(8,128)} fusion(f32[8,8,32,128]{3,2,1,0:T(8,128)} %bitcast.17, f32[8,32,128]{2,1,0:T(8,128)S(1)} %copy-done.1), kind=kLoop, calls=%fused_computation | loop fusion | flops 262144 | bytes 2228224 | tf_op jit(solution)/shard_map/mul | solution.py:871
  137.9 0.0 copy-done.3
  137.9 0.6 copy.14
Async XLA Ops:
  0.6 0.7 copy-start.7
  0.6 0.7 copy-start.4
  0.7 0.7 copy-start.5
  0.7 0.7 copy-start.6
  1.9 1.0 copy-start.2
  2.9 1.0 copy-start
  6.2 129.3 %copy-start.1 = (f32[8,32,128]{2,1,0:T(8,128)S(1)}, f32[8,32,128]{2,1,0:T(8,128)}, u32[]{:S(2)}) copy-start(f32[8,32,128]{2,1,0:T(8,128)} %param.10) | copy-start | bytes 393220
  135.5 2.3 %copy-start.3 = (f32[32,32]{1,0:T(8,128)S(1)}, f32[32,32]{1,0:T(8,128)}, u32[]{:S(2)}) copy-start(f32[32,32]{1,0:T(8,128)} %get-tuple-element.9) | copy-start | bytes 12292

commit v2 on v1

--- a/solution.py
+++ b/solution.py
@@ -201,13 +201,11 @@
     tables,
     src_in,
     pm_in,
-    obs_in,
     bs_in,
     adj,
     r_out,
     src_all,
     pm_all,
-    obs_all,
     out_all,
     gat,
     ycol,
@@ -234,14 +232,16 @@
     eb,
     fb,
     we,
-    pm_send,
-    pm_recv,
-    fw_send,
-    fw_recv,
+    col_send,
+    col_recv,
+    row_send,
+    row_recv,
+    dir_send,
+    dir_recv,
+    core_send,
+    core_recv,
     src_send,
     src_recv,
-    obs_send,
-    obs_recv,
     ret_send,
     ret_recv,
     y_send,
@@ -254,15 +254,17 @@
 ):
     nt, nd, nx, ny, cells = dims
     rows = nx * ny
-    half = rows // 2
     quarter = rows // nd
+    piece = 3 * quarter
     pitch = rows + PAD
-    pm_pitch = 2 * rows + PAD
+    pm_pitch = 3 * rows + PAD
     gpitch = quarter + PAD
     me = lax.axis_index("tile")
     q = lax.axis_index("dir")
     core = lax.rem(q, 2)
     partner = q + 1 - 2 * core
+    across = lax.rem(q + nd // 2, nd)
+    mate = me + 1 - 2 * lax.rem(me, 2)
 
     def span(start, size):
         return pl.ds(pl.multiple_of(start, 8), size)
@@ -292,14 +294,49 @@
             device_id_type=MESH,
         )
 
-    def pm_copy(k, owner, to):
+    def place(owner, part):
+        return pm_all.at[span(owner * pm_pitch + part * piece, piece)]
+
+    mine = pm_in.at[span(q * piece, piece)]
+
+    def col_copy(k, owner, to):
+        return remote(mine, place(owner, q), col_send.at[k], col_recv.at[k], "tile", to)
+
+    def row_copy(k, base, to):
+        owner = lax.rem(base + nt - k, nt)
         return remote(
-            pm_in.at[span(core * rows, rows)],
-            pm_all.at[span(owner * pm_pitch + core * rows, rows)],
-            pm_send.at[k],
-            pm_recv.at[k],
+            mine if k == 0 else place(owner, q),
+            place(owner, q),
+            row_send.at[k],
+            row_recv.at[k],
             "tile",
             to,
+        )
+
+    def holder(k):
+        return behind(k) if k % 2 == 0 else lax.rem(mate + nt - (k - 1), nt)
+
+    def dir_copy(k, part):
+        owner = holder(k)
+        return remote(
+            mine if k == 0 else place(owner, q),
+            place(owner, part),
+            dir_send.at[k],
+            dir_recv.at[k],
+            "dir",
+            across,
+        )
+
+    def core_copy(k, slot, part):
+        owner = holder(k)
+        source = mine if k == 0 and slot == 0 else place(owner, part)
+        return remote(
+            source,
+            place(owner, part),
+            core_send.at[slot, k],
+            core_recv.at[slot, k],
+            "dir",
+            partner,
         )
 
     def src_copy(k, owner, to):
@@ -312,41 +349,41 @@
             to,
         )
 
-    def obs_copy(k, owner, to):
-        return remote(
-            obs_in, obs_all.at[span(owner * pitch, rows)], obs_send.at[k], obs_recv.at[k], "tile", to
-        )
-
-    def fw_copy(k, which):
-        owner = behind(k)
-        place = pm_all.at[span(owner * pm_pitch + which * rows, rows)]
-        source = pm_in.at[span(which * rows, rows)] if k == 0 else place
-        return remote(source, place, fw_send.at[k], fw_recv.at[k], "dir", partner)
-
-    for k in range(1, nt):
-        pm_copy(k, me, ahead(k)).start()
-    for k in range(1, nt):
+    evens = range(2, nt, 2)
+    for k in evens:
+        col_copy(k, me, ahead(k)).start()
+    row_copy(0, me, mate).start()
+    dir_copy(0, q).start()
+    core_copy(0, 0, q).start()
+    for k in evens:
         src_copy(k, me, ahead(k)).start()
     own = [
-        pltpu.make_async_copy(
-            pm_in.at[span(core * rows, rows)],
-            pm_all.at[span(me * pm_pitch + core * rows, rows)],
-            own_sem.at[0],
-        ),
+        pltpu.make_async_copy(mine, place(me, q), own_sem.at[0]),
         pltpu.make_async_copy(
             src_in.at[span(me * rows, rows)], src_all.at[span(me * pitch, rows)], own_sem.at[1]
         ),
-        pltpu.make_async_copy(obs_in, obs_all.at[span(me * pitch, rows)], own_sem.at[2]),
     ]
     for copy in own:
         copy.start()
-    fw_copy(0, core).start()
-    for k in range(1, nt):
-        pm_copy(k, behind(k), behind(k)).wait_recv()
-        fw_copy(k, core).start()
+    for k in evens:
+        col_copy(k, behind(k), behind(k)).wait_recv()
+        row_copy(k, me, mate).start()
+        dir_copy(k, q).start()
+        core_copy(k, 0, q).start()
+    for k in range(1, nt, 2):
+        src_copy(k, me, ahead(k)).start()
+    for k in range(0, nt, 2):
+        row_copy(k, mate, mate).wait_recv()
+        dir_copy(k + 1, q).start()
+        core_copy(k + 1, 0, q).start()
+    sent = list(range(0, nt, 2)) + list(range(1, nt, 2))
+    for k in sent:
+        dir_copy(k, across).wait_recv()
+        core_copy(k, 1, across).start()
     own[0].wait()
-    for k in range(nt):
-        fw_copy(k, 1 - core).wait_recv()
+    for k in sent:
+        core_copy(k, 0, partner).wait_recv()
+        core_copy(k, 1, lax.rem(partner + nd // 2, nd)).wait_recv()
 
     sub = lax.broadcasted_iota(jnp.int32, (SUBL, LANES), 0)
     lane = lax.broadcasted_iota(jnp.int32, (SUBL, LANES), 1)
@@ -374,15 +411,17 @@
     def planes(step, init):
         return lax.fori_loop(0, nx, step, init)
 
-    half_planes = nx // 2
+    part_planes = nx // nd
+
+    def table_row(x):
+        block = x // part_planes
+        return block * piece + (x - block * part_planes) * ny
 
     def lookup(x, _):
-        block = x // half_planes
-        inside = x - block * half_planes
-        base = block * rows + inside * ny
+        base = table_row(x)
         for y in range(ny):
             perm_f[x + 1, y] = pm_all[pl.ds(base + y, SUBL, stride=pm_pitch), :]
-            mat = pm_all[pl.ds(base + half + y, SUBL, stride=pm_pitch), :]
+            mat = pm_all[pl.ds(base + quarter + y, SUBL, stride=pm_pitch), :]
             storage, alpha, bulk, shear = zero, zero, zero, zero
             for c in range(NCLASS):
                 hit = mat == float(c)
@@ -535,8 +574,6 @@
     for k in range(1, nt):
         src_copy(k, behind(k), behind(k)).wait_recv()
     own[1].wait()
-    for k in range(1, nt):
-        obs_copy(k, me, ahead(k)).start()
 
     def take_source(x, _):
         for y in range(ny):
@@ -628,14 +665,11 @@
 
         @pl.when(turn == 0)
         def _():
-            for k in range(1, nt):
-                obs_copy(k, behind(k), behind(k)).wait_recv()
-            own[2].wait()
-
             def last_press(x, _):
+                base = table_row(x) + 2 * quarter
                 for y in range(ny):
                     p = pb[x + 1, y] + c0 * r0[x + 1, y] + a1 * r1[x + 1, y]
-                    r0[x + 1, y] = p * obs_all[pl.ds(x * ny + y, SUBL, stride=pitch), :]
+                    r0[x + 1, y] = p * pm_all[pl.ds(base + y, SUBL, stride=pm_pitch), :]
                 return 0
 
             planes(last_press, 0)
@@ -756,13 +790,17 @@
         mat = mat - (mat[:, j : j + 1] / root) * row
 
     for k in range(1, nt):
-        pm_copy(k, me, ahead(k)).wait_send()
         src_copy(k, me, ahead(k)).wait_send()
-        obs_copy(k, me, ahead(k)).wait_send()
         for m in order:
             ret_copy(m, k, me, ahead(k)).wait_send()
     for k in range(nt):
-        fw_copy(k, core).wait_send()
+        if k % 2 == 0:
+            row_copy(k, me, mate).wait_send()
+        if k in evens:
+            col_copy(k, me, ahead(k)).wait_send()
+        dir_copy(k, q).wait_send()
+        core_copy(k, 0, q).wait_send()
+        core_copy(k, 1, across).wait_send()
         for m in order[:-1]:
             to = lax.rem(q + m, nd)
             y_copy(m, k, q, to, to).wait_send()
@@ -784,15 +822,16 @@
     rows = nx * ny
     tables = jnp.stack([class_storage, class_alpha, class_bulk, class_shear])
     source = (base_sens * probes).reshape(count * rows, nz)
+    quarter = rows // nd
     coefs = jnp.stack(
         [
-            perm.reshape(2, rows // 2, nz),
-            material.astype(jnp.float32).reshape(2, rows // 2, nz),
+            perm.reshape(nd, quarter, nz),
+            material.astype(jnp.float32).reshape(nd, quarter, nz),
+            obs_weight.reshape(nd, quarter, nz),
         ],
         axis=1,
-    ).reshape(2 * rows, nz)
+    ).reshape(3 * rows, nz)
     nall = nd * count
-    quarter = rows // nd
     vmem = pl.BlockSpec(memory_space=pltpu.VMEM)
     f32 = jnp.float32
 
@@ -809,8 +848,7 @@
     inner_f, outer_f = field(nx), field(nx + 2)
     scratch = [
         rowbuf(nt * (rows + PAD)),
-        rowbuf(nt * (2 * rows + PAD)),
-        rowbuf(nt * (rows + PAD)),
+        rowbuf(nt * (3 * rows + PAD)),
         rowbuf(nt * (rows + PAD)),
         rowbuf(nall * (quarter + PAD)),
         pltpu.VMEM((nall, quarter * nz), f32),
@@ -843,6 +881,8 @@
         sems((nt,)),
         sems((nt,)),
         sems((nt,)),
+        sems((2, nt)),
+        sems((2, nt)),
         sems((nt,)),
         sems((nt,)),
         sems((nd, nt)),
@@ -861,20 +901,20 @@
             jax.ShapeDtypeStruct((count * rows, nz), f32),
             jax.ShapeDtypeStruct((nall, nall), f32),
         ),
-        in_specs=[pl.BlockSpec(memory_space=pltpu.SMEM)] + [vmem] * 4,
+        in_specs=[pl.BlockSpec(memory_space=pltpu.SMEM)] + [vmem] * 3,
         out_specs=(vmem, vmem),
         scratch_shapes=scratch,
         compiler_params=pltpu.CompilerParams(
             collective_id=0, has_side_effects=True, vmem_limit_bytes=60 * 1024 * 1024
         ),
-    )(tables, source, coefs, obs_weight.reshape(rows, nz), base_sens.reshape(rows, nz))
+    )(tables, source, coefs, base_sens.reshape(rows, nz))
     return (base_sens * adjoint.reshape(probes.shape), r_factor)
 
 
 def body(probes, *others):
     nt, nd = lax.axis_size("tile"), lax.axis_size("dir")
     count, nx, ny, nz = probes.shape
-    fits = nt == SUBL and count == nt and nz == LANES and nd % 2 == 0 and nx % 2 == 0
+    fits = nt == SUBL and count == nt and nz == LANES and nd == 4 and nx % nd == 0
     fits = fits and ny % 8 == 0 and (nx * ny) % (8 * nd) == 0 and nd * nt <= LANES
     fits = fits and nx * ny * nz <= 32768
     return (local_body if fits else halo_body)(probes, *others)

time: 139 us -> 119 us (0.86)
  Pallas kernels: 129 us -> 110 us
    pallas_call x1, Pallas kernels: 129 us -> 110 us  [local_body(): pl.pallas_call(functools.partial(kernel, (nt, nd, nx, ny, float(nt * rows...]
where the time goes in v2:
time: 119 us
  Pallas kernels  110 us (92%)
  other arithmetic  6.99 us (6%)
  local copies, waits for them, and re-layouts  1.5 us (1%)
    pallas_call x1, Pallas kernels, local_body(): pl.pallas_call(functools.partial(kernel, (nt, nd, nx, ny, float(nt * rows...  110 us

profile of v2, /device:TPU:0, one launch (start us, length us, event | category | flops | bytes accessed | tf_op | source)
XLA Modules:
  0.0 119.1 jit_solution(3360653209950403498)
XLA Ops:
  0.6 0.0 copy-start.8
  0.6 0.0 copy-start.5
  0.7 0.0 copy-start.6
  0.7 0.0 copy-start.7
  0.7 0.6 copy-done.8
  1.3 0.0 copy-done.5
  1.3 0.0 copy-done.6
  1.3 0.0 copy-done.7
  1.3 0.6 pad_maximum_fusion.1.tables
  1.9 0.0 copy-start.2
  1.9 0.0 copy-start.3
  1.9 1.0 convert_element_type.3
  2.9 0.0 copy-done.2
  2.9 0.1 copy-done.3
  3.0 0.0 copy-start
  3.0 0.8 pad_maximum_fusion
  3.7 0.2 copy-done
  3.9 2.3 %broadcast_multiply_fusion.1 = f32[8,8,32,128]{3,2,1,0:T(8,128)} fusion(f32[8,8,32,128]{3,2,1,0:T(8,128)} %param.9, f32[8,32,128]{2,1,0:T(8,128)S(1)} %copy-done), kind=kLoop, calls=%fused_computation.1 | loop fusion | flops 262144 | bytes 2228224 | tf_op jit(solution)/shard_map/mul | solution.py:824
  6.2 0.0 copy-start.1
  6.2 109.9 %shard_map.104 = (f32[2048,128]{1,0:T(8,128)}, f32[32,32]{1,0:T(8,128)}) custom-call(f32[4,8]{1,0:T(4,128)} %pad_maximum_fusion.1.tables, f32[2048,128]{1,0:T(8,128)} %bitcast.17, f32[768,128]{1,0:T(8,128)} %bitcast.18, f32[256,128]{1,0:T(8,128)} %bitcast.19), custom_call_target="tpu_custom_call" | custom-call | tf_op jit(solution)/shard_map/pallas_call | solution.py:898
  116.1 0.0 copy-done.1
  116.2 0.0 copy-start.4
  116.2 2.3 %broadcast_multiply_fusion = f32[8,8,32,128]{3,2,1,0:T(8,128)} fusion(f32[8,8,32,128]{3,2,1,0:T(8,128)} %bitcast.20, f32[8,32,128]{2,1,0:T(8,128)S(1)} %copy-done.1), kind=kLoop, calls=%fused_computation | loop fusion | flops 262144 | bytes 2228224 | tf_op jit(solution)/shard_map/mul | solution.py:911
  118.5 0.0 copy-done.4
  118.5 0.6 copy.15
Async XLA Ops:
  0.6 0.7 copy-start.8
  0.6 0.7 copy-start.5
  0.7 0.7 copy-start.6
  0.7 0.7 copy-start.7
  1.9 1.0 copy-start.2
  1.9 1.0 copy-start.3
  3.0 1.0 copy-start
  6.2 109.9 %copy-start.1 = (f32[8,32,128]{2,1,0:T(8,128)S(1)}, f32[8,32,128]{2,1,0:T(8,128)}, u32[]{:S(2)}) copy-start(f32[8,32,128]{2,1,0:T(8,128)} %param.10) | copy-start | bytes 393220
  116.2 2.3 %copy-start.4 = (f32[32,32]{1,0:T(8,128)S(1)}, f32[32,32]{1,0:T(8,128)}, u32[]{:S(2)}) copy-start(f32[32,32]{1,0:T(8,128)} %get-tuple-element.9) | copy-start | bytes 12292

commit v3 on v2

--- a/solution.py
+++ b/solution.py
@@ -199,11 +199,12 @@
 def kernel(
     dims,
     tables,
-    src_in,
+    probes_in,
     pm_in,
     bs_in,
     adj,
     r_out,
+    src_in,
     src_all,
     pm_all,
     out_all,
@@ -275,6 +276,15 @@
     def behind(k):
         return lax.rem(me + nt - k, nt)
 
+    def scale_source(r, _):
+        scale = bs_in[span(r * SUBL, SUBL), :]
+        for d in range(nt):
+            at = span(d * rows + r * SUBL, SUBL)
+            src_in[at, :] = probes_in[at, :] * scale
+        return 0
+
+    lax.fori_loop(0, rows // SUBL, scale_source, 0)
+
     barrier = pltpu.get_barrier_semaphore()
     for k in range(1, nt):
         pl.semaphore_signal(barrier, inc=1, device_id={"tile": ahead(k)}, device_id_type=MESH)
@@ -821,7 +831,7 @@
     count, nx, ny, nz = probes.shape
     rows = nx * ny
     tables = jnp.stack([class_storage, class_alpha, class_bulk, class_shear])
-    source = (base_sens * probes).reshape(count * rows, nz)
+    source = probes.reshape(count * rows, nz)
     quarter = rows // nd
     coefs = jnp.stack(
         [
@@ -847,6 +857,7 @@
     sems = pltpu.SemaphoreType.DMA
     inner_f, outer_f = field(nx), field(nx + 2)
     scratch = [
+        rowbuf(count * rows),
         rowbuf(nt * (rows + PAD)),
         rowbuf(nt * (3 * rows + PAD)),
         rowbuf(nt * (rows + PAD)),

time: 119 us -> 117 us (0.983)
  other arithmetic: 6.99 us -> 4.65 us
    mul x1 -> x0, other arithmetic: 2.32 us -> none  [local_body(): source = (base_sens * probes).reshape(count * rows, nz)]
where the time goes in v3:
time: 117 us
  Pallas kernels  110 us (94%)
  other arithmetic  4.65 us (4%)
  local copies, waits for them, and re-layouts  1.34 us (1%)
    pallas_call x1, Pallas kernels, local_body(): pl.pallas_call(functools.partial(kernel, (nt, nd, nx, ny, float(nt * rows...  110 us

profile of v3, /device:TPU:0, one launch (start us, length us, event | category | flops | bytes accessed | tf_op | source)
XLA Modules:
  0.0 116.8 jit_solution(9075643200829844912)
XLA Ops:
  0.6 0.0 copy-start.7
  0.6 0.0 copy-start.4
  0.7 0.0 copy-start.5
  0.7 0.0 copy-start.6
  0.7 0.6 copy-done.7
  1.3 0.0 copy-done.4
  1.3 0.0 copy-done.5
  1.3 0.0 copy-done.6
  1.3 0.6 pad_maximum_fusion.1.tables
  1.9 0.0 copy-start.1
  1.9 0.0 copy-start.2
  1.9 1.0 convert_element_type.3
  2.9 0.0 copy-done.1
  2.9 0.1 copy-done.2
  3.0 0.8 pad_maximum_fusion
  3.7 0.0 copy-start
  3.7 110.2 %shard_map.104 = (f32[2048,128]{1,0:T(8,128)}, f32[32,32]{1,0:T(8,128)}) custom-call(f32[4,8]{1,0:T(4,128)} %pad_maximum_fusion.1.tables, f32[2048,128]{1,0:T(8,128)} %bitcast.18, f32[768,128]{1,0:T(8,128)} %bitcast.17, f32[256,128]{1,0:T(8,128)} %bitcast.20), custom_call_target="tpu_custom_call" | custom-call | tf_op jit(solution)/shard_map/pallas_call | solution.py:909
  113.9 0.0 copy-done
  113.9 0.0 copy-start.3
  113.9 2.3 %broadcast_multiply_fusion = f32[8,8,32,128]{3,2,1,0:T(8,128)} fusion(f32[8,8,32,128]{3,2,1,0:T(8,128)} %bitcast.19, f32[8,32,128]{2,1,0:T(8,128)S(1)} %copy-done), kind=kLoop, calls=%fused_computation | loop fusion | flops 262144 | bytes 2228224 | tf_op jit(solution)/shard_map/mul | solution.py:922
  116.2 0.0 copy-done.3
  116.2 0.6 copy.15
Async XLA Ops:
  0.6 0.7 copy-start.7
  0.6 0.7 copy-start.4
  0.7 0.7 copy-start.5
  0.7 0.7 copy-start.6
  1.9 1.0 copy-start.1
  1.9 1.0 copy-start.2
  3.7 110.2 %copy-start = (f32[8,32,128]{2,1,0:T(8,128)S(1)}, f32[8,32,128]{2,1,0:T(8,128)}, u32[]{:S(2)}) copy-start(f32[8,32,128]{2,1,0:T(8,128)} %param.10) | copy-start | bytes 393220
  113.9 2.3 %copy-start.3 = (f32[32,32]{1,0:T(8,128)S(1)}, f32[32,32]{1,0:T(8,128)}, u32[]{:S(2)}) copy-start(f32[32,32]{1,0:T(8,128)} %get-tuple-element.9) | copy-start | bytes 12292
